TPU v7x, 512 devices: a whole 4x4x16 slice. The times are simulated.
512 devices in a mesh: seq: 128 (over x_lo, y, z), mp: 4 (over x_hi, core).
Axes of the slice: x: 4 (x_hi: 2, x_lo: 2; x = x_hi * 2 + x_lo), y: 4, z: 16, core: 2. Of those that a mesh axis runs over, the one named last changes fastest.
Arguments:
- incoming_image_patches: bfloat16 [1, 128, 128, 1152], P(None, 'seq', 'mp'), may hold values from -6 to 6
- initial_standardize_scaling: float32 [1152], replicated, may hold values from 0.1 to 1.9
- acceptance_matrix: bfloat16 [1152, 1024], P(None, 'mp'), may hold values from -0.1875 to 0.1875
- addressing_matrix: bfloat16 [1152, 1024], P(None, 'mp'), may hold values from -0.1875 to 0.1875
- content_matrix: bfloat16 [1152, 1024], P(None, 'mp'), may hold values from -0.1875 to 0.1875
- forgetting_lowdim_left_factor: bfloat16 [1152, 64], replicated, may hold values from -0.1875 to 0.1875
- forgetting_lowdim_right_factor: bfloat16 [64, 1024], P(None, 'mp'), may hold values from -1.5 to 1.5
- forgetting_baseline: float32 [1024], P('mp'), may hold values from -6 to 1
- self_token_reward: float32 [1024], P('mp'), may hold values from -3 to 3
- horizontal_cluster_scaling: float32 [1024], P('mp'), may hold values from 0.1 to 1.9
- vertical_cluster_scaling: float32 [1024], P('mp'), may hold values from 0.1 to 1.9
- temporal_mix_projection_matrix: bfloat16 [1024, 1152], P('mp'), may hold values from -0.1875 to 0.1875
- later_standardize_scaling: float32 [1152], replicated, may hold values from 0.1 to 1.9
- feature_mix_addressing_matrix: bfloat16 [1152, 4608], P('seq', 'mp'), may hold values from -0.1875 to 0.1875
- feature_mix_content_matrix: bfloat16 [4608, 1152], P('mp', 'seq'), may hold values from -0.09375 to 0.09375
Outputs:
- block_out: bfloat16 [1, 128, 128, 1152], P(None, 'seq', 'mp')
All inputs are finite; a program needn't handle non-finite values.
Results may differ from a plain program's by a relative error of at most 0.017.
Values may be sent and summed in bfloat16 or wider, within the bound.
No kernel may reach another device: no remote copies, remote signals or barrier semaphores. Data moves between devices by JAX's collectives and lax.ppermute only.
A program may use at most 64 MiB of HBM per device.

v0:
```python
import jax
import jax.numpy as jnp
from jax import lax
from jax.sharding import Mesh
from jax.sharding import PartitionSpec as P

SUBSPACE_SIZE = 64
SEQ = ("x_lo", "y", "z")
MP = ("x_hi", "core")
PLANE = ("x_lo", "y")


def from_everyone(value, axis):
    copies = jnp.broadcast_to(value, (lax.axis_size(axis), *value.shape))
    return lax.all_to_all(copies, axis, split_axis=0, concat_axis=0, tiled=True)


def split_up(value, dim, size):
    lengths = value.shape
    pieces = value.reshape(*lengths[:dim], size, lengths[dim] // size, *lengths[dim + 1 :])
    return jnp.moveaxis(pieces, dim, 0)


def sent_and_summed(value, axis, dim):
    size = lax.axis_size(axis)
    pieces = lax.all_to_all(split_up(value, dim, size), axis, 0, 0, tiled=True)
    return jnp.sum(pieces.astype(jnp.float32), axis=0)


def layer_norm(inputs, gain):
    values = inputs.astype(jnp.float32)
    average = jnp.mean(values, axis=-1, keepdims=True)
    centred = values - average
    spread = jnp.mean(centred * centred, axis=-1, keepdims=True)
    return (centred * lax.rsqrt(spread + 1e-05) * gain).astype(jnp.bfloat16)


def heads_first(array, nheads):
    number, length, inner_width = array.shape
    shaped = array.astype(jnp.float32).reshape(number, length, nheads, inner_width // nheads)
    return shaped.transpose(0, 2, 1, 3)


def recurrence(recept_in, keying_in, decays_in, valued_in, boost_in, gain):
    number, length, inner_width = recept_in.shape
    nheads = inner_width // SUBSPACE_SIZE
    head_size = inner_width // nheads
    blocks = length // 16
    acceptance_horizontal_lines = heads_first(recept_in, nheads)
    addressing_horizontal_lines = heads_first(keying_in, nheads)
    decays = heads_first(decays_in, nheads)
    content_horizontal_lines = heads_first(valued_in, nheads)
    boost = boost_in.reshape(nheads, 1, head_size)
    running = jnp.cumsum(decays, axis=2)
    before = running - decays
    before_blocks = before.reshape(number, nheads, blocks, 16, head_size)
    anchor = before_blocks[:, :, :, :1, :]
    queries = acceptance_horizontal_lines.reshape(number, nheads, blocks, 16, head_size) * jnp.exp(
        before_blocks - anchor
    )
    places = jnp.arange(length)
    limits = (jnp.arange(blocks) + 1) * 16
    usable = places[None, :] < limits[:, None]
    exponent = anchor - running[:, :, None, :, :]
    exponent = jnp.where(usable[None, None, :, :, None], exponent, -10000.0)
    weighted = addressing_horizontal_lines[:, :, None, :, :] * jnp.exp(exponent)
    scores = jnp.einsum("nhbqc,nhbsc->nhbqs", queries, weighted, precision=lax.Precision.HIGHEST)
    query_places = places.reshape(blocks, 16)
    earlier = places[None, None, :] < query_places[:, :, None]
    scores = jnp.where(earlier[None, None], scores, 0.0)
    current = jnp.sum(acceptance_horizontal_lines * boost * addressing_horizontal_lines, axis=-1)
    summed = jnp.einsum(
        "nhbqs,nhsc->nhbqc", scores, content_horizontal_lines, precision=lax.Precision.HIGHEST
    )
    summed = (
        summed.reshape(number, nheads, length, head_size)
        + current[..., None] * content_horizontal_lines
    )
    average = jnp.mean(summed, axis=-1, keepdims=True)
    centred = summed - average
    spread = jnp.mean(centred * centred, axis=-1, keepdims=True)
    normed = (
        (centred * lax.rsqrt(spread + 0.00064))
        .transpose(0, 2, 1, 3)
        .reshape(number, length, inner_width)
    )
    return (normed * gain).astype(jnp.bfloat16)


def unit_order(planes, depth, width):
    stored = jnp.arange(planes * depth * width)
    z, rest = (stored // (planes * width), stored % (planes * width))
    plane, row = (rest // width, rest % width)
    true_place = (plane * depth + z) * width + row
    return true_place


def shards(
    incoming_image_patches,
    initial_standardize_scaling,
    acceptance_matrix,
    addressing_matrix,
    content_matrix,
    forgetting_lowdim_left_factor,
    forgetting_lowdim_right_factor,
    forgetting_baseline,
    self_token_reward,
    horizontal_cluster_scaling,
    vertical_cluster_scaling,
    temporal_mix_projection_matrix,
    later_standardize_scaling,
    feature_mix_addressing_matrix,
    feature_mix_content_matrix,
):
    images, row_count, part_cols, model_width = incoming_image_patches.shape
    tokens = incoming_image_patches.reshape(part_cols, model_width)
    whole_rows = lax.all_gather(tokens, MP, axis=0, tiled=True)
    full_cols = whole_rows.shape[0]
    inner_width = acceptance_matrix.shape[1]
    planes, depth = (lax.axis_size(PLANE), lax.axis_size("z"))
    width = feature_mix_addressing_matrix.shape[0]
    pair = jnp.stack([feature_mix_addressing_matrix, feature_mix_content_matrix.T])
    plane_pair = from_everyone(pair, PLANE).reshape(planes, *pair.shape)
    plane_up = plane_pair[:, 0].reshape(planes * width, -1)
    plane_down = plane_pair[:, 1].reshape(planes * width, -1)
    full_up = lax.all_gather(plane_up, "z", axis=0, tiled=True)
    full_down = lax.all_gather(plane_down, "z", axis=0, tiled=True)
    xn1 = layer_norm(whole_rows, initial_standardize_scaling)
    recept = jnp.dot(xn1, acceptance_matrix, preferred_element_type=jnp.float32).astype(
        jnp.bfloat16
    )
    keying = jnp.dot(xn1, addressing_matrix, preferred_element_type=jnp.float32).astype(
        jnp.bfloat16
    )
    valued = jnp.dot(xn1, content_matrix, preferred_element_type=jnp.float32).astype(jnp.bfloat16)
    latent = jnp.tanh(
        jnp.dot(xn1, forgetting_lowdim_left_factor, preferred_element_type=jnp.float32)
    ).astype(jnp.bfloat16)
    decay = (
        -0.7
        * jax.nn.sigmoid(
            forgetting_baseline
            + jnp.dot(latent, forgetting_lowdim_right_factor, preferred_element_type=jnp.float32)
        )
    ).astype(jnp.bfloat16)
    row_out = recurrence(
        recept[None],
        keying[None],
        decay[None],
        valued[None],
        self_token_reward,
        horizontal_cluster_scaling,
    )[0]
    sent = jnp.stack([recept, keying, decay, row_out], axis=1)
    got = lax.all_to_all(
        sent.reshape(full_cols, 4 * inner_width // 128, 128),
        SEQ,
        split_axis=0,
        concat_axis=0,
        tiled=True,
    )
    height = got.shape[0]
    got = got.reshape(height, 4, inner_width)
    col_out = recurrence(
        got[None, :, 0],
        got[None, :, 1],
        got[None, :, 2],
        got[None, :, 3],
        self_token_reward,
        vertical_cluster_scaling,
    )[0]
    back = lax.all_to_all(
        col_out.reshape(height, inner_width // 128, 128),
        SEQ,
        split_axis=0,
        concat_axis=0,
        tiled=True,
    ).reshape(full_cols, inner_width)
    partial_value = jnp.dot(
        back, temporal_mix_projection_matrix, preferred_element_type=jnp.float32
    ).astype(jnp.bfloat16)
    attended = sent_and_summed(partial_value, MP, 0)
    residual = (tokens.astype(jnp.float32) + attended).astype(jnp.bfloat16)
    mix_input = layer_norm(residual, later_standardize_scaling)
    places = unit_order(planes, depth, width)
    moved = (jnp.arange(model_width)[:, None] == places[None, :]).astype(jnp.bfloat16)
    mix_input = jnp.dot(mix_input, moved, preferred_element_type=jnp.float32).astype(jnp.bfloat16)
    mix_all = lax.all_gather(mix_input, MP, axis=0, tiled=True)
    hidden_pre = jnp.dot(mix_all, full_up, preferred_element_type=jnp.float32)
    positive = jnp.maximum(hidden_pre, 0.0)
    hidden = (positive * positive).astype(jnp.bfloat16)
    downward = lax.dot_general(
        hidden, full_down, (((1,), (1,)), ((), ())), preferred_element_type=jnp.float32
    ).astype(jnp.bfloat16)
    downward = lax.dot_general(
        downward, moved, (((1,), (1,)), ((), ())), preferred_element_type=jnp.float32
    ).astype(jnp.bfloat16)
    mixed = sent_and_summed(downward, MP, 0)
    block_out = (residual.astype(jnp.float32) + mixed).astype(jnp.bfloat16)
    return block_out.reshape(images, row_count, part_cols, model_width)


def solution(mesh):
    torus = Mesh(mesh.devices.reshape(2, 4, 16, 2, 2), (*SEQ, *MP))
    return jax.shard_map(
        shards,
        mesh=torus,
        in_specs=(
            P(None, SEQ, MP, None),
            P(),
            P(None, MP),
            P(None, MP),
            P(None, MP),
            P(),
            P(None, MP),
            P(MP),
            P(MP),
            P(MP),
            P(MP),
            P(MP, None),
            P(),
            P(SEQ, MP),
            P(MP, SEQ),
        ),
        out_specs=P(None, SEQ, MP, None),
        check_vma=False,
    )
```

profile of v0, /device:TPU:1, one launch (start us, length us, event | category | flops | bytes accessed | tf_op | source)
XLA Modules:
  0.0 206.6 jit_solution(17887059847881086414)
XLA Ops:
  6.6 0.0 all-gather.4.cloned.1.call-start
  6.6 0.9 pad_maximum_fusion.1
  7.5 0.2 broadcast_in_dim.42
  7.7 12.3 %all_to_all.25 = bf16[8,2,9,1152]{3,1,2,0:T(2,128)(2,1)S(1)} all-to-all(bf16[8,2,9,1152]{3,1,2,0:T(2,128)(2,1)S(1)} %broadcast_in_dim.42), channel_id=1, replica_groups=mesh['x_lo'=2,'y'=4,'z'=16,'x_hi'=2,'core'=2] {'x_lo','y'}, dimensions={0} | all-to-all | bytes 663552 | tf_op jit(solution)/shard_map/all_to_all | solution.py:15
  20.1 1.5 slice_reduce_fusion
  21.6 0.0 copy-start.5
  21.6 0.7 reshape_squeeze.7
  22.3 0.0 all-gather.4.cloned.1.call-update
  22.4 11.8 %all-gather = bf16[1,1,128,1152]{3,2,1,0:T(8,128)(2,1)S(1)} all-gather(bf16[1,1,32,1152]{3,2,1,0:T(8,128)(2,1)S(1)} %copy-done.1), channel_id=2, replica_groups=mesh['x_lo'=2,'y'=4,'z'=16,'x_hi'=2,'core'=2] {'x_hi','core'}, dimensions={2}, use_global_device_ids=true | all-gather | bytes 368640 | tf_op jit(solution)/shard_map/all_gather | solution.py:117
  34.2 0.1 convert_reduce_fusion
  34.3 0.2 fusion.26
  34.6 0.0 copy-start.6
  34.6 0.5 fusion.13
  35.2 0.1 copy.93
  35.3 0.1 copy.94
  35.4 0.3 reduce_window_sum.17
  35.7 0.1 copy.96
  35.9 0.3 convolution_convert_fusion.4
  36.2 0.1 copy.91
  36.3 0.1 copy.92
  36.4 0.0 copy-start.4
  36.4 0.3 convolution_convert_fusion.3
  36.8 0.1 copy.95
  36.9 1.4 convolution_convert_fusion.2
  38.3 0.1 copy.97
  38.4 0.1 iota_compare_fusion.8
  38.5 0.1 iota_compare_fusion.7
  38.6 1.2 convolution_select_fusion.1
  39.8 0.2 fusion.94
  40.1 0.1 copy.98
  40.2 0.1 mul.219
  40.3 0.1 multiply_reduce_fusion.2
  40.5 0.1 copy.99
  40.7 0.2 copy.100
  40.9 0.9 copy.101
  41.8 15.7 %all-to-all-start = ((bf16[128,8,128]{2,1,0:T(8,128)(2,1)}), bf16[128,8,128]{2,1,0:T(8,128)(2,1)S(1)}, u32[]{:S(2)}, u32[]{:S(2)}) async-start(bf16[128,8,128]{2,1,0:T(8,128)(2,1)} %copy.101), calls=%async_computation | async-start | bytes 524288 | tf_op jit(solution)/shard_map/all_to_all | solution.py:155
  57.5 0.0 all-gather.6.cloned.1.call-start
  57.5 0.8 reshape_squeeze.8
  58.3 0.0 all-gather.6.cloned.1.call-update
  58.3 22.2 %all-to-all-done = bf16[128,8,128]{2,1,0:T(8,128)(2,1)S(1)} async-done(((bf16[128,8,128]{2,1,0:T(8,128)(2,1)}), bf16[128,8,128]{2,1,0:T(8,128)(2,1)S(1)}, u32[]{:S(2)}, u32[]{:S(2)}) %all-to-all-start) | async-done | bytes 262176 | tf_op jit(solution)/shard_map/all_to_all | solution.py:155
  80.5 0.2 copy.102
  80.8 0.1 copy.104
  80.9 0.3 reduce_window_sum.18
  81.2 0.1 copy.105
  81.3 0.1 copy.103
  81.5 1.2 convolution_select_fusion
  82.7 0.2 fusion.95
  83.0 0.1 copy.106
  83.1 0.1 fusion.55
  83.4 0.1 copy.107
  83.5 0.1 copy.108
  83.6 22.7 %all_to_all.26 = bf16[128,2,128]{2,1,0:T(2,128)(2,1)S(1)} all-to-all(bf16[128,2,128]{2,1,0:T(2,128)(2,1)S(1)} %copy.108), channel_id=1, replica_groups=mesh['x_lo'=2,'y'=4,'z'=16,'x_hi'=2,'core'=2] {'x_lo','y','z'}, dimensions={0} | all-to-all | bytes 131072 | tf_op jit(solution)/shard_map/all_to_all | solution.py:172
  106.3 1.0 convolution_convert_fusion.1
  107.2 7.1 %all-to-all-start.2 = ((bf16[4,32,1152]{2,1,0:T(8,128)(2,1)}), bf16[4,32,1152]{2,1,0:T(8,128)(2,1)S(1)}, u32[]{:S(2)}, u32[]{:S(2)}) async-start(bf16[4,32,1152]{2,1,0:T(8,128)(2,1)} %bitcast.53), calls=%async_computation.2 | async-start | bytes 589824 | tf_op jit(solution)/shard_map/all_to_all | solution.py:26
  114.3 6.9 %all-to-all-done.2 = bf16[4,32,1152]{2,1,0:T(8,128)(2,1)S(1)} async-done(((bf16[4,32,1152]{2,1,0:T(8,128)(2,1)}), bf16[4,32,1152]{2,1,0:T(8,128)(2,1)S(1)}, u32[]{:S(2)}, u32[]{:S(2)}) %all-to-all-start.2) | async-done | bytes 294944 | tf_op jit(solution)/shard_map/all_to_all | solution.py:26
  121.2 0.1 convert_reduce_fusion.3
  121.4 0.2 fusion.47
  121.6 1.1 fusion.7
  122.7 8.2 %all_gather.13 = bf16[128,1152]{1,0:T(8,128)(2,1)S(1)} all-gather(bf16[32,1152]{1,0:T(8,128)(2,1)S(1)} %fusion.7), channel_id=1, replica_groups=mesh['x_lo'=2,'y'=4,'z'=16,'x_hi'=2,'core'=2] {'x_hi','core'}, dimensions={0}, use_global_device_ids=true | all-gather | bytes 368640 | tf_op jit(solution)/shard_map/all_gather | solution.py:188
  130.9 2.4 %fusion.5 = bf16[128,1152]{1,0:T(8,128)(2,1)S(1)} fusion(bf16[128,1152]{1,0:T(8,128)(2,1)S(1)} %all_gather.13, bf16[1152,1152]{1,0:T(8,128)(2,1)} %all-gather.4.cloned.1.call-done), kind=kOutput, calls=%fused_computation.7 | convolution fusion | flops 340180992 | bytes 3244032 | tf_op jit(solution)/shard_map/dot_general | solution.py:189
  133.3 40.7 %all-gather.6.cloned.1.call-done = bf16[1152,1152]{1,0:T(8,128)(2,1)} async-done(((bf16[72,1152]{1,0:T(8,128)(2,1)}), bf16[1152,1152]{1,0:T(8,128)(2,1)}) %all-gather.6.cloned.1.call-update) | async-done | bytes 2654224 | tf_op jit(solution)/shard_map/all_gather | solution.py:127
  174.0 3.7 %fusion.6 = bf16[128,1152]{1,0:T(8,128)(2,1)S(1)} fusion(s32[1152]{0:T(1024)S(1)} %fusion.74, bf16[128,1152]{1,0:T(8,128)(2,1)S(1)} %fusion.5, bf16[1152,1152]{1,0:T(8,128)(2,1)} %all-gather.6.cloned.1.call-done), kind=kOutput, calls=%fused_computation.8 | convolution fusion | flops 681099264 | bytes 3248640 | tf_op jit(solution)/shard_map/dot_general | solution.py:195
  177.6 21.4 %all_to_all.27 = bf16[4,32,1152]{2,1,0:T(8,128)(2,1)S(1)} all-to-all(bf16[4,32,1152]{2,1,0:T(8,128)(2,1)S(1)} %bitcast.162), channel_id=1, replica_groups=mesh['x_lo'=2,'y'=4,'z'=16,'x_hi'=2,'core'=2] {'x_hi','core'}, dimensions={0} | all-to-all | bytes 589824 | tf_op jit(solution)/shard_map/all_to_all | solution.py:26
  199.1 0.7 fusion.53
  (50 shorter events, 0.7 us)
Async XLA Ops:
  6.5 99.7 %copy-start = (bf16[256,1152]{1,0:T(8,128)(2,1)S(1)}, bf16[256,1152]{1,0:T(8,128)(2,1)}, u32[]{:S(2)}) copy-start(bf16[256,1152]{1,0:T(8,128)(2,1)} %param.26) | copy-start | bytes 1769476
  6.5 15.8 %copy-start.1 = (bf16[1,1,32,1152]{3,2,1,0:T(8,128)(2,1)S(1)}, bf16[1,1,32,1152]{3,2,1,0:T(8,128)(2,1)}, u32[]{:S(2)}) copy-start(bf16[1,1,32,1152]{3,2,1,0:T(8,128)(2,1)} %param.15) | copy-start | bytes 221188
  6.5 28.0 %copy-start.9 = (f32[1152]{0:T(1024)S(1)}, f32[1152]{0:T(1024)}, u32[]{:S(2)}) copy-start(f32[1152]{0:T(1024)} %param.16) | copy-start | bytes 13828
  6.5 28.0 %copy-start.7 = (bf16[1152,64]{0,1:T(8,128)(2,1)S(1)}, bf16[1152,64]{0,1:T(8,128)(2,1)}, u32[]{:S(2)}) copy-start(bf16[1152,64]{0,1:T(8,128)(2,1)} %param.20) | copy-start | bytes 442372
  6.5 28.1 %copy-start.8 = (bf16[64,256]{1,0:T(8,128)(2,1)S(1)}, bf16[64,256]{1,0:T(8,128)(2,1)}, u32[]{:S(2)}) copy-start(bf16[64,256]{1,0:T(8,128)(2,1)} %param.21) | copy-start | bytes 98308
  6.5 28.1 %copy-start.11 = (f32[256]{0:T(256)S(1)}, f32[256]{0:T(256)}, u32[]{:S(2)}) copy-start(f32[256]{0:T(256)} %param.22) | copy-start | bytes 3076
  6.6 124.3 %all-gather.4.cloned.1.call-start = ((), (), s32[]{:S(2)}) async-start(), calls=%async_computation.5 | async-start | bytes 2820096 | tf_op jit(solution)/shard_map/all_gather | solution.py:126
  21.6 14.3 %copy-start.5 = (bf16[1152,256]{1,0:T(8,128)(2,1)S(1)}, bf16[1152,256]{1,0:T(8,128)(2,1)}, u32[]{:S(2)}) copy-start(bf16[1152,256]{1,0:T(8,128)(2,1)} %param.17) | copy-start | bytes 1769476
  34.6 1.8 copy-start.6
  36.4 3.7 %copy-start.4 = (f32[256]{0:T(256)S(1)}, f32[256]{0:T(256)}, u32[]{:S(2)}) copy-start(f32[256]{0:T(256)} %param.23) | copy-start | bytes 3076
  36.9 3.8 %copy-start.2 = (f32[256]{0:T(256)S(1)}, f32[256]{0:T(256)}, u32[]{:S(2)}) copy-start(f32[256]{0:T(256)} %param.24) | copy-start | bytes 3076
  41.8 38.7 %all-to-all-start = ((bf16[128,8,128]{2,1,0:T(8,128)(2,1)}), bf16[128,8,128]{2,1,0:T(8,128)(2,1)S(1)}, u32[]{:S(2)}, u32[]{:S(2)}) async-start(bf16[128,8,128]{2,1,0:T(8,128)(2,1)} %copy.101), calls=%async_computation | async-start | bytes 524288 | tf_op jit(solution)/shard_map/all_to_all | solution.py:155
  57.5 116.5 %all-gather.6.cloned.1.call-start = ((), (), s32[]{:S(2)}) async-start(), calls=%async_computation.6 | async-start | bytes 2820096 | tf_op jit(solution)/shard_map/all_gather | solution.py:127
  81.2 2.3 %copy-start.3 = (f32[256]{0:T(256)S(1)}, f32[256]{0:T(256)}, u32[]{:S(2)}) copy-start(f32[256]{0:T(256)} %param.25) | copy-start | bytes 3076
  82.7 38.9 %copy-start.10 = (f32[1152]{0:T(1024)S(1)}, f32[1152]{0:T(1024)}, u32[]{:S(2)}) copy-start(f32[1152]{0:T(1024)} %param.27) | copy-start | bytes 13828
  107.2 14.0 %all-to-all-start.2 = ((bf16[4,32,1152]{2,1,0:T(8,128)(2,1)}), bf16[4,32,1152]{2,1,0:T(8,128)(2,1)S(1)}, u32[]{:S(2)}, u32[]{:S(2)}) async-start(bf16[4,32,1152]{2,1,0:T(8,128)(2,1)} %bitcast.53), calls=%async_computation.2 | async-start | bytes 589824 | tf_op jit(solution)/shard_map/all_to_all | solution.py:26
Sparse Core Ops, SparseCore 0:
  22.5 78.9 all-gather.3
  103.5 70.3 all-gather.5
where the time goes:
time: 207 us
  blocking collectives  76.4 us (37%)
  waiting for transfers between devices  69.8 us (34%)
  starting transfers between devices  22.8 us (11%)
  between operations  13.9 us (7%)
  matrix products  13.6 us (7%)
  local copies, waits for them, and re-layouts  6.29 us (3%)
  other arithmetic  3.71 us (2%)
    all_gather x1, waiting for transfers between devices, shards(): full_down = lax.all_gather(plane_down, 'z', axis=0, tiled=True)  40.7 us
    all_to_all x1, blocking collectives, shards(): lax.all_to_all(col_out.reshape(height, inner_width // 128, 128), SEQ, spl...  22.7 us
    all_to_all x1, waiting for transfers between devices, shards(): lax.all_to_all(sent.reshape(full_cols, 4 * inner_width // 128, 128), SEQ,...  22.2 us
    all_to_all x1, blocking collectives, sent_and_summed(): pieces = lax.all_to_all(split_up(value, dim, size), axis, 0, 0, tiled=True)  21.4 us
    all_to_all x1, starting transfers between devices, shards(): lax.all_to_all(sent.reshape(full_cols, 4 * inner_width // 128, 128), SEQ,...  15.7 us
    all_to_all x1, blocking collectives, from_everyone(): return lax.all_to_all(copies, axis, split_axis=0, concat_axis=0, tiled=True)  12.3 us
    all_gather x1, blocking collectives, shards(): whole_rows = lax.all_gather(tokens, MP, axis=0, tiled=True)  11.8 us
    all_gather x1, blocking collectives, shards(): mix_all = lax.all_gather(mix_input, MP, axis=0, tiled=True)  8.17 us
  transfers between devices with their start and end apart: 4, of which 3 were waited for; matrix products, arithmetic and copies ran while one was open for 8% of the time, Pallas kernels for 0%

commit v1 on v0

--- a/solution.py
+++ b/solution.py
@@ -114,7 +114,11 @@
 ):
     images, row_count, part_cols, model_width = incoming_image_patches.shape
     tokens = incoming_image_patches.reshape(part_cols, model_width)
-    whole_rows = lax.all_gather(tokens, MP, axis=0, tiled=True)
+    z1 = tuple((tokens for _ in range(lax.psum(1, axis_name=MP))))
+    t1 = jnp.stack(z1)
+    whole_rows = jnp.concatenate(
+        lax.all_to_all(t1, concat_axis=0, axis_name=MP, split_axis=0), axis=0
+    )
     full_cols = whole_rows.shape[0]
     inner_width = acceptance_matrix.shape[1]
     planes, depth = (lax.axis_size(PLANE), lax.axis_size("z"))

time: 207 us -> 215 us (1.039)
  blocking collectives: 76.4 us -> 51.4 us
  waiting for transfers between devices: 69.8 us -> 84 us
  starting transfers between devices: 22.8 us -> 36.3 us
  local copies, waits for them, and re-layouts: 6.29 us -> 11.2 us
    all_to_all x0 -> x2, starting transfers between devices: none -> 14.8 us  [the longest x1 8.84 us: shards(): lax.all_to_all(t1, concat_axis=0, axis_name=MP, split_axis=0)]
    all_to_all x1 -> x0, blocking collectives: 12.3 us -> none  [from_everyone(): return lax.all_to_all(copies, axis, split_axis=0, concat_axis=0, tiled=True)]
    all_gather x1 -> x0, blocking collectives: 11.8 us -> none  [shards(): whole_rows = lax.all_gather(tokens, MP, axis=0, tiled=True)]
    all_to_all x0 -> x2, waiting for transfers between devices: none -> 10 us  [the longest x1 5.5 us: from_everyone(): return lax.all_to_all(copies, axis, split_axis=0, concat_axis=0, tiled=True)]
    all_gather x1, waiting for transfers between devices: 40.7 us -> 44.4 us  [shards(): full_down = lax.all_gather(plane_down, 'z', axis=0, tiled=True)]
  transfers between devices with their start and end apart: 4 -> 6, of which waited for: 3 -> 5; matrix products, arithmetic and copies ran while one was open for 8% -> 9% of each run, Pallas kernels for 0% -> 0%
where the time goes in v1:
time: 215 us; the launch traced here: 214 us
  waiting for transfers between devices  84 us (39%)
  blocking collectives  51.4 us (24%)
  starting transfers between devices  36.3 us (17%)
  between operations  14 us (7%)
  matrix products  13.2 us (6%)
  local copies, waits for them, and re-layouts  11.2 us (5%)
  other arithmetic  3.91 us (2%)
    all_gather x1, waiting for transfers between devices, shards(): full_down = lax.all_gather(plane_down, 'z', axis=0, tiled=True)  44.4 us
    all_to_all x1, waiting for transfers between devices, shards(): lax.all_to_all(sent.reshape(full_cols, 4 * inner_width // 128, 128), SEQ,...  22.7 us
    all_to_all x1, blocking collectives, shards(): lax.all_to_all(col_out.reshape(height, inner_width // 128, 128), SEQ, spl...  21.8 us
    all_to_all x1, blocking collectives, sent_and_summed(): pieces = lax.all_to_all(split_up(value, dim, size), axis, 0, 0, tiled=True)  21.4 us
    all_to_all x1, starting transfers between devices, shards(): lax.all_to_all(sent.reshape(full_cols, 4 * inner_width // 128, 128), SEQ,...  15.1 us
    all_to_all x1, starting transfers between devices, shards(): lax.all_to_all(t1, concat_axis=0, axis_name=MP, split_axis=0)  8.84 us
    all_gather x1, blocking collectives, shards(): mix_all = lax.all_gather(mix_input, MP, axis=0, tiled=True)  8.17 us
    all_to_all x1, waiting for transfers between devices, sent_and_summed(): pieces = lax.all_to_all(split_up(value, dim, size), axis, 0, 0, tiled=True)  6.87 us
  transfers between devices with their start and end apart: 6, of which 5 were waited for; matrix products, arithmetic and copies ran while one was open for 9% of the time, Pallas kernels for 0%

profile of v1, /device:TPU:1, one launch (start us, length us, event | category | flops | bytes accessed | tf_op | source)
XLA Modules:
  0.0 213.9 jit_solution(10251653952551385043)
XLA Ops:
  6.5 0.9 pad_maximum_fusion.1
  7.5 0.9 broadcast_in_dim.42
  8.4 5.9 %all-to-all-start.4 = ((bf16[8,2,9,1152]{3,1,2,0:T(2,128)(2,1)}), bf16[8,2,9,1152]{3,1,2,0:T(2,128)(2,1)S(1)}, u32[]{:S(2)}, u32[]{:S(2)}) async-start(bf16[8,2,9,1152]{3,1,2,0:T(2,128)(2,1)} %broadcast_in_dim.42), calls=%async_computation.4 | async-start | bytes 663552 | tf_op jit(solution)/shard_map/all_to_all | solution.py:15
  14.3 0.8 mul.220
  15.1 0.1 iota_compare_fusion.7
  15.2 5.5 %all-to-all-done.4 = bf16[8,2,9,1152]{3,1,2,0:T(2,128)(2,1)S(1)} async-done(((bf16[8,2,9,1152]{3,1,2,0:T(2,128)(2,1)}), bf16[8,2,9,1152]{3,1,2,0:T(2,128)(2,1)S(1)}, u32[]{:S(2)}, u32[]{:S(2)}) %all-to-all-start.4) | async-done | bytes 331808 | tf_op jit(solution)/shard_map/all_to_all | solution.py:15
  20.7 1.6 stack.24
  22.3 8.8 %all-to-all-start = ((bf16[4,32,1152]{2,1,0:T(8,128)(2,1)}), bf16[4,32,1152]{2,1,0:T(8,128)(2,1)S(1)}, u32[]{:S(2)}, u32[]{:S(2)}) async-start(bf16[4,32,1152]{2,1,0:T(8,128)(2,1)} %stack.24), calls=%async_computation | async-start | bytes 589824 | tf_op jit(solution)/shard_map/all_to_all | solution.py:120
  31.1 1.5 slice_reduce_fusion
  32.7 0.7 reshape_squeeze.7
  33.4 0.1 iota_compare_fusion.8
  33.5 4.5 %all-to-all-done = bf16[4,32,1152]{2,1,0:T(8,128)(2,1)S(1)} async-done(((bf16[4,32,1152]{2,1,0:T(8,128)(2,1)}), bf16[4,32,1152]{2,1,0:T(8,128)(2,1)S(1)}, u32[]{:S(2)}, u32[]{:S(2)}) %all-to-all-start) | async-done | bytes 294944 | tf_op jit(solution)/shard_map/all_to_all | solution.py:120
  38.0 0.1 convert_reduce_fusion.2
  38.2 0.1 div.52
  38.2 0.2 multiply_reduce_fusion
  38.5 0.1 rsqrt.36
  38.6 0.2 fusion.25
  38.8 0.5 fusion.13
  39.3 0.1 copy.111
  39.4 0.1 copy.112
  39.6 0.4 copy-done.7
  39.9 0.3 reduce_window_sum.17
  40.2 0.7 copy-done.5
  41.0 0.8 copy.114
  41.7 0.3 convolution_convert_fusion.4
  42.0 0.1 copy.109
  42.1 0.1 copy.110
  42.3 0.3 convolution_convert_fusion.3
  42.5 0.1 copy.113
  42.7 0.3 convolution_convert_fusion.2
  42.9 0.1 copy.115
  43.0 2.1 convolution_select_fusion.1
  45.2 0.3 fusion.83
  45.4 0.1 copy.116
  45.6 0.1 multiply_reduce_fusion.3
  45.8 0.1 copy.117
  46.0 0.2 copy.118
  46.2 0.9 copy.119
  47.1 15.1 %all-to-all-start.1 = ((bf16[128,8,128]{2,1,0:T(8,128)(2,1)}), bf16[128,8,128]{2,1,0:T(8,128)(2,1)S(1)}, u32[]{:S(2)}, u32[]{:S(2)}) async-start(bf16[128,8,128]{2,1,0:T(8,128)(2,1)} %copy.119), calls=%async_computation.1 | async-start | bytes 524288 | tf_op jit(solution)/shard_map/all_to_all | solution.py:159
  62.2 0.8 reshape_squeeze.8
  63.0 22.7 %all-to-all-done.1 = bf16[128,8,128]{2,1,0:T(8,128)(2,1)S(1)} async-done(((bf16[128,8,128]{2,1,0:T(8,128)(2,1)}), bf16[128,8,128]{2,1,0:T(8,128)(2,1)S(1)}, u32[]{:S(2)}, u32[]{:S(2)}) %all-to-all-start.1) | async-done | bytes 262176 | tf_op jit(solution)/shard_map/all_to_all | solution.py:159
  85.7 0.2 copy.120
  86.0 0.1 copy.122
  86.1 0.3 reduce_window_sum.18
  86.5 0.1 copy.123
  86.6 0.1 copy.121
  86.7 1.2 convolution_select_fusion
  88.0 0.2 fusion.84
  88.2 0.1 copy.124
  88.3 0.1 fusion.50
  88.6 0.1 copy.125
  88.8 21.8 %all_to_all.30 = bf16[128,2,128]{2,1,0:T(2,128)(2,1)S(1)} all-to-all(bf16[128,2,128]{2,1,0:T(2,128)(2,1)S(1)} %copy.126), channel_id=1, replica_groups=mesh['x_lo'=2,'y'=4,'z'=16,'x_hi'=2,'core'=2] {'x_lo','y','z'}, dimensions={0} | all-to-all | bytes 131072 | tf_op jit(solution)/shard_map/all_to_all | solution.py:176
  110.6 1.0 convolution_convert_fusion.1
  111.6 6.4 %all-to-all-start.3 = ((bf16[4,32,1152]{2,1,0:T(8,128)(2,1)}), bf16[4,32,1152]{2,1,0:T(8,128)(2,1)S(1)}, u32[]{:S(2)}, u32[]{:S(2)}) async-start(bf16[4,32,1152]{2,1,0:T(8,128)(2,1)} %bitcast.54), calls=%async_computation.3 | async-start | bytes 589824 | tf_op jit(solution)/shard_map/all_to_all | solution.py:26
  118.0 6.9 %all-to-all-done.3 = bf16[4,32,1152]{2,1,0:T(8,128)(2,1)S(1)} async-done(((bf16[4,32,1152]{2,1,0:T(8,128)(2,1)}), bf16[4,32,1152]{2,1,0:T(8,128)(2,1)S(1)}, u32[]{:S(2)}, u32[]{:S(2)}) %all-to-all-start.3) | async-done | bytes 294944 | tf_op jit(solution)/shard_map/all_to_all | solution.py:26
  124.9 0.1 convert_reduce_fusion.3
  125.1 0.2 fusion.44
  125.3 1.1 fusion.7
  126.4 8.2 %all_gather.9 = bf16[128,1152]{1,0:T(8,128)(2,1)S(1)} all-gather(bf16[32,1152]{1,0:T(8,128)(2,1)S(1)} %fusion.7), channel_id=1, replica_groups=mesh['x_lo'=2,'y'=4,'z'=16,'x_hi'=2,'core'=2] {'x_hi','core'}, dimensions={0}, use_global_device_ids=true | all-gather | bytes 368640 | tf_op jit(solution)/shard_map/all_gather | solution.py:192
  134.6 2.4 %fusion.5 = bf16[128,1152]{1,0:T(8,128)(2,1)S(1)} fusion(bf16[128,1152]{1,0:T(8,128)(2,1)S(1)} %all_gather.9, bf16[1152,1152]{1,0:T(8,128)(2,1)} %all-gather.3.cloned.1.call-done), kind=kOutput, calls=%fused_computation.7 | convolution fusion | flops 340180992 | bytes 3244032 | tf_op jit(solution)/shard_map/dot_general | solution.py:193
  137.0 44.4 %all-gather.5.cloned.1.call-done = bf16[1152,1152]{1,0:T(8,128)(2,1)} async-done(((bf16[72,1152]{1,0:T(8,128)(2,1)}), bf16[1152,1152]{1,0:T(8,128)(2,1)}) %all-gather.5.cloned.1.call-update) | async-done | bytes 2654224 | tf_op jit(solution)/shard_map/all_gather | solution.py:131
  181.3 3.7 %fusion.6 = bf16[128,1152]{1,0:T(8,128)(2,1)S(1)} fusion(s32[1152]{0:T(1024)S(1)} %fusion.69, bf16[128,1152]{1,0:T(8,128)(2,1)S(1)} %fusion.5, bf16[1152,1152]{1,0:T(8,128)(2,1)} %all-gather.5.cloned.1.call-done), kind=kOutput, calls=%fused_computation.8 | convolution fusion | flops 681099264 | bytes 3248640 | tf_op jit(solution)/shard_map/dot_general | solution.py:199
  185.0 21.4 %all_to_all.31 = bf16[4,32,1152]{2,1,0:T(8,128)(2,1)S(1)} all-to-all(bf16[4,32,1152]{2,1,0:T(8,128)(2,1)S(1)} %bitcast.156), channel_id=1, replica_groups=mesh['x_lo'=2,'y'=4,'z'=16,'x_hi'=2,'core'=2] {'x_hi','core'}, dimensions={0} | all-to-all | bytes 589824 | tf_op jit(solution)/shard_map/all_to_all | solution.py:26
  206.4 0.7 fusion.47
  (64 shorter events, 0.8 us)
Async XLA Ops:
  6.5 104.1 %copy-start = (bf16[256,1152]{1,0:T(8,128)(2,1)S(1)}, bf16[256,1152]{1,0:T(8,128)(2,1)}, u32[]{:S(2)}) copy-start(bf16[256,1152]{1,0:T(8,128)(2,1)} %param.26) | copy-start | bytes 1769476
  6.5 32.0 %copy-start.9 = (f32[1152]{0:T(1024)S(1)}, f32[1152]{0:T(1024)}, u32[]{:S(2)}) copy-start(f32[1152]{0:T(1024)} %param.16) | copy-start | bytes 13828
  7.4 31.4 %copy-start.12 = (bf16[1152,64]{0,1:T(8,128)(2,1)S(1)}, bf16[1152,64]{0,1:T(8,128)(2,1)}, u32[]{:S(2)}) copy-start(bf16[1152,64]{0,1:T(8,128)(2,1)} %param.20) | copy-start | bytes 442372
  7.4 31.4 %copy-start.13 = (bf16[64,256]{1,0:T(8,128)(2,1)S(1)}, bf16[64,256]{1,0:T(8,128)(2,1)}, u32[]{:S(2)}) copy-start(bf16[64,256]{1,0:T(8,128)(2,1)} %param.21) | copy-start | bytes 98308
  7.4 31.4 %copy-start.15 = (f32[256]{0:T(256)S(1)}, f32[256]{0:T(256)}, u32[]{:S(2)}) copy-start(f32[256]{0:T(256)} %param.22) | copy-start | bytes 3076
  8.4 12.3 %all-to-all-start.4 = ((bf16[8,2,9,1152]{3,1,2,0:T(2,128)(2,1)}), bf16[8,2,9,1152]{3,1,2,0:T(2,128)(2,1)S(1)}, u32[]{:S(2)}, u32[]{:S(2)}) async-start(bf16[8,2,9,1152]{3,1,2,0:T(2,128)(2,1)} %broadcast_in_dim.42), calls=%async_computation.4 | async-start | bytes 663552 | tf_op jit(solution)/shard_map/all_to_all | solution.py:15
  22.3 15.7 %all-to-all-start = ((bf16[4,32,1152]{2,1,0:T(8,128)(2,1)}), bf16[4,32,1152]{2,1,0:T(8,128)(2,1)S(1)}, u32[]{:S(2)}, u32[]{:S(2)}) async-start(bf16[4,32,1152]{2,1,0:T(8,128)(2,1)} %stack.24), calls=%async_computation | async-start | bytes 589824 | tf_op jit(solution)/shard_map/all_to_all | solution.py:120
  31.1 103.5 %all-gather.3.cloned.1.call-start = ((), (), s32[]{:S(2)}) async-start(), calls=%async_computation.6 | async-start | bytes 2820096 | tf_op jit(solution)/shard_map/all_gather | solution.py:130
  32.6 9.1 %copy-start.2 = (bf16[1152,256]{1,0:T(8,128)(2,1)S(1)}, bf16[1152,256]{1,0:T(8,128)(2,1)}, u32[]{:S(2)}) copy-start(bf16[1152,256]{1,0:T(8,128)(2,1)} %param.17) | copy-start | bytes 1769476
  38.6 3.7 %copy-start.3 = (bf16[1152,256]{1,0:T(8,128)(2,1)S(1)}, bf16[1152,256]{1,0:T(8,128)(2,1)}, u32[]{:S(2)}) copy-start(bf16[1152,256]{1,0:T(8,128)(2,1)} %param.18) | copy-start | bytes 1769476
  39.3 0.6 copy-start.7
  39.3 3.3 %copy-start.4 = (bf16[1152,256]{1,0:T(8,128)(2,1)S(1)}, bf16[1152,256]{1,0:T(8,128)(2,1)}, u32[]{:S(2)}) copy-start(bf16[1152,256]{1,0:T(8,128)(2,1)} %param.19) | copy-start | bytes 1769476
  40.2 0.7 copy-start.5
  41.7 1.3 copy-start.6
  42.5 3.4 %copy-start.10 = (f32[256]{0:T(256)S(1)}, f32[256]{0:T(256)}, u32[]{:S(2)}) copy-start(f32[256]{0:T(256)} %param.24) | copy-start | bytes 3076
  42.6 3.3 %copy-start.8 = (bf16[128,256]{1,0:T(8,128)(2,1)S(1)}, bf16[128,256]{1,0:T(8,128)(2,1)}, u32[]{:S(2)}) copy-start(bf16[128,256]{1,0:T(8,128)(2,1)} %copy-done.7) | copy-start | bytes 196612
  47.1 38.7 %all-to-all-start.1 = ((bf16[128,8,128]{2,1,0:T(8,128)(2,1)}), bf16[128,8,128]{2,1,0:T(8,128)(2,1)S(1)}, u32[]{:S(2)}, u32[]{:S(2)}) async-start(bf16[128,8,128]{2,1,0:T(8,128)(2,1)} %copy.119), calls=%async_computation.1 | async-start | bytes 524288 | tf_op jit(solution)/shard_map/all_to_all | solution.py:159
  62.2 119.1 %all-gather.5.cloned.1.call-start = ((), (), s32[]{:S(2)}) async-start(), calls=%async_computation.7 | async-start | bytes 2820096 | tf_op jit(solution)/shard_map/all_gather | solution.py:131
  86.4 2.3 %copy-start.11 = (f32[256]{0:T(256)S(1)}, f32[256]{0:T(256)}, u32[]{:S(2)}) copy-start(f32[256]{0:T(256)} %param.25) | copy-start | bytes 3076
  87.9 37.0 %copy-start.1 = (bf16[1,1,32,1152]{3,2,1,0:T(8,128)(2,1)S(1)}, bf16[1,1,32,1152]{3,2,1,0:T(8,128)(2,1)}, u32[]{:S(2)}) copy-start(bf16[1,1,32,1152]{3,2,1,0:T(8,128)(2,1)} %param.15) | copy-start | bytes 221188
  88.0 37.3 %copy-start.14 = (f32[1152]{0:T(1024)S(1)}, f32[1152]{0:T(1024)}, u32[]{:S(2)}) copy-start(f32[1152]{0:T(1024)} %param.27) | copy-start | bytes 13828
  111.6 13.3 %all-to-all-start.3 = ((bf16[4,32,1152]{2,1,0:T(8,128)(2,1)}), bf16[4,32,1152]{2,1,0:T(8,128)(2,1)S(1)}, u32[]{:S(2)}, u32[]{:S(2)}) async-start(bf16[4,32,1152]{2,1,0:T(8,128)(2,1)} %bitcast.54), calls=%async_computation.3 | async-start | bytes 589824 | tf_op jit(solution)/shard_map/all_to_all | solution.py:26
Sparse Core Ops, SparseCore 0:
  34.0 74.0 all-gather.2
  110.2 71.0 all-gather.4
